TPU v7x, 32 devices: a whole 2x2x4 slice. The times are simulated.
32 devices in a mesh: dp: 4 (over y, x), vocab: 8 (over z, core).
Axes of the slice: x: 2, y: 2, z: 4, core: 2. Of those that a mesh axis runs over, the one named last changes fastest.
Arguments:
- hidden: bfloat16 [4, 32, 3584], P('dp', None, 'vocab'), may hold values from -6 to 6
- kl_hidden: bfloat16 [4, 32, 3584], P('dp', None, 'vocab'), may hold values from -6 to 6
- head_weight: bfloat16 [256000, 3584], P(('dp', 'vocab')), may hold values from -0.3125 to 0.3125
- labels: int32 [4, 32], P('dp'), may hold values from 0 to 255999
- token_mask: int32 [4, 32], P('dp'), may hold values 0 or 1
- kl_pair: int32 [4], P('dp'), may hold values from 0 to 3, as said below
- desirable: int32 [4], P('dp'), may hold values 0 or 1
- ref_logps: float32 [4, 64], P('dp', 'vocab'), may hold values from -23 to -11
Outputs:
- token_logps: float32 [4, 64], P('dp', 'vocab')
- seq_losses: float32 [4], P('dp')
- loss: float32 [], replicated
Inputs may be any that keep to these rules, and one draw needn't show every extreme that they name: kl_pair is a permutation of the 4 sequences with kl_pair[s] != s.
All inputs are finite; a program needn't handle non-finite values. No bound on the sum of `token_mask` or of `desirable` on one device may be relied on, other than what follows from the above.
Results may differ from a plain program's by a relative error of at most 0.0003.
Values may be sent and summed in bfloat16 or wider, within the bound.
A program may use at most 128 MiB of HBM per device.

v0:
```python
import jax
import jax.numpy as jnp
from jax import lax
from jax.sharding import PartitionSpec as P

kto_beta = 0.1
desirable_weight = 1.0
undesirable_weight = 1.33


def label_terms(logits, targets, first_row):
    shifted = targets - first_row
    inside = (shifted >= 0) & (shifted < logits.shape[1])
    clipped = jnp.clip(shifted, 0, logits.shape[1] - 1)
    picked = jnp.take_along_axis(logits, clipped[:, None], axis=1)[:, 0]
    return (jnp.sum(jnp.exp(logits), axis=1), jnp.where(inside, picked, 0.0))


def kto_losses(logratio, kl_total, seq_total, desirable):
    kl_estimate = kl_total / seq_total
    wanted = desirable_weight * (1.0 - jax.nn.sigmoid(kto_beta * (logratio - kl_estimate)))
    unwanted = undesirable_weight * (1.0 - jax.nn.sigmoid(kto_beta * (kl_estimate - logratio)))
    return jnp.where(desirable == 1, wanted, unwanted)


def on_device(hidden, kl_hidden, head_weight, labels, token_mask, kl_pair, desirable, ref_logps):
    sub_seq = hidden.shape[0]
    length = hidden.shape[1]
    vocab_rows = head_weight.shape[0]
    model_width = head_weight.shape[1]
    groups = lax.axis_size("vocab")
    vocab_index = lax.axis_index("vocab")
    data_index = lax.axis_index("dp")
    first_row = (data_index * groups + vocab_index) * vocab_rows
    all_labels, all_masks, all_pairs, all_desirable = (
        lax.all_gather(labels, "dp", axis=0, tiled=True),
        lax.all_gather(token_mask, "dp", axis=0, tiled=True),
        lax.all_gather(kl_pair, "dp", axis=0, tiled=True),
        lax.all_gather(desirable, "dp", axis=0, tiled=True),
    )
    targets = jnp.concatenate([all_labels, all_labels[all_pairs]], axis=1)
    weights_mask = jnp.concatenate([all_masks, all_masks[all_pairs]], axis=1).astype(jnp.float32)
    seq_total = targets.shape[0]
    columns = targets.shape[1]
    combined = jnp.concatenate([hidden, kl_hidden], axis=1)
    whole_rows = lax.all_gather(combined, "vocab", axis=2, tiled=True)
    portion = lax.all_gather(whole_rows, "dp", axis=0, tiled=True)
    number = portion.shape[0]
    logits = lax.dot_general(
        portion.reshape(number * columns, model_width),
        head_weight,
        (((1,), (1,)), ((), ())),
        preferred_element_type=jnp.float32,
    )
    portion_targets = targets.reshape(-1)
    part_sum, part_pick = label_terms(logits, portion_targets, first_row)
    token_stats = jnp.stack(
        [part_sum.reshape(number, columns), part_pick.reshape(number, columns)], axis=1
    )
    partition = token_stats[:, 0]
    picked = token_stats[:, 1]
    own_cols = columns // groups
    row_start = data_index * sub_seq
    col_start = vocab_index * own_cols
    ref_full = lax.dynamic_update_slice(
        jnp.zeros((seq_total, columns), jnp.float32), ref_logps, (row_start, col_start)
    )
    partition, picked, ref_all = lax.psum((partition, picked, ref_full), ("dp", "vocab"))
    token_logps = picked - jnp.log(partition)
    differences = weights_mask * (token_logps - ref_all)
    logratio = jnp.sum(differences[:, :length], axis=1)
    kl_terms = jnp.sum(differences[:, length:], axis=1)
    losses = kto_losses(logratio, jnp.sum(kl_terms), seq_total, all_desirable)
    own_logps = lax.dynamic_slice(token_logps, (row_start, col_start), (sub_seq, own_cols))
    own_losses = lax.dynamic_slice_in_dim(losses, row_start, sub_seq, 0)
    return (own_logps, own_losses, jnp.mean(losses))


def solution(mesh):
    in_specs = (
        P("dp", None, "vocab"),
        P("dp", None, "vocab"),
        P(("dp", "vocab"), None),
        P("dp", None),
        P("dp", None),
        P("dp"),
        P("dp"),
        P("dp", "vocab"),
    )
    out_specs = (P("dp", "vocab"), P("dp"), P())
    return jax.shard_map(
        on_device, mesh=mesh, in_specs=in_specs, out_specs=out_specs, check_vma=False
    )
```

profile of v0, /device:TPU:0, one launch (start us, length us, event | category | flops | bytes accessed | tf_op | source)
XLA Modules:
  0.0 153.6 jit_solution(2589287121122592298)
XLA Ops:
  7.2 0.0 all-gather.4.cloned.1.call-start
  7.2 0.8 pad_maximum_fusion
  8.0 0.2 copy.14
  8.2 23.7 %all_gather.20 = bf16[1,64,3584]{1,0,2:T(2,128)(2,1)S(1)} all-gather(bf16[1,64,448]{1,0,2:T(2,128)(2,1)S(1)} %copy.14), channel_id=1, replica_groups=mesh['dp'=4,'vocab'=8] {'vocab'}, dimensions={2}, use_global_device_ids=true | all-gather | bytes 516096 | tf_op jit(solution)/shard_map/all_gather | solution.py:46
  31.8 3.1 %copy.15 = bf16[1,64,3584]{2,1,0:T(8,128)(2,1)} copy(bf16[1,64,3584]{1,0,2:T(2,128)(2,1)S(1)} %all_gather.20) | data formatting | bytes 917504 | tf_op jit(solution)/shard_map/all_gather | solution.py:46
  34.9 0.0 all-gather.4.cloned.1.call-update
  36.2 1.2 dynamic-slice
  37.5 0.8 dynamic-update-slice
  38.3 0.8 dynamic-update-slice.1
  39.0 7.4 %all-reduce.2 = (s32[4]{0:T(128)S(1)}, s32[4]{0:T(128)S(1)}) all-reduce(s32[4]{0:T(128)S(1)} %dynamic-update-slice, s32[4]{0:T(128)S(1)} %dynamic-update-slice.1), channel_id=1, replica_groups=mesh['dp'=4,'vocab'=8] {'dp'}, use_global_device_ids=true, to_apply=%add | all-reduce | flops 8 | bytes 64
  46.4 7.9 %all-gather.1 = s32[4,1,32]{2,1,0:T(1,128)S(1)} all-gather(s32[1,1,32]{2,1,0:T(1,128)} %bitcast.17), channel_id=1, replica_groups=mesh['dp'=4,'vocab'=8] {'dp'}, dimensions={0}, use_global_device_ids=true | all-gather | bytes 640 | tf_op jit(solution)/shard_map/all_gather | solution.py:37
  54.3 0.6 gather_fusion.1
  54.9 7.2 %all-gather = s32[4,1,32]{2,1,0:T(1,128)S(1)} all-gather(s32[1,1,32]{2,1,0:T(1,128)} %bitcast.18), channel_id=1, replica_groups=mesh['dp'=4,'vocab'=8] {'dp'}, dimensions={0}, use_global_device_ids=true | all-gather | bytes 640 | tf_op jit(solution)/shard_map/all_gather | solution.py:36
  62.1 0.6 gather_fusion
  62.7 0.1 broadcast_clamp_fusion
  62.8 0.1 min.12
  62.8 0.8 dynamic_update_slice.3
  63.7 4.1 %all-gather.4.cloned.1.call-done = bf16[4,64,3584]{2,1,0:T(8,128)(2,1)} async-done(((bf16[1,64,3584]{2,1,0:T(8,128)(2,1)}), bf16[4,64,3584]{2,1,0:T(8,128)(2,1)}) %all-gather.4.cloned.1.call-update) | async-done | bytes 1835024 | tf_op jit(solution)/shard_map/all_gather | solution.py:47
  67.7 25.9 %exponential_reduce_fusion = (f32[256]{0:T(256)S(1)}, f32[256,8000]{0,1:T(8,128)}) fusion(bf16[256,3584]{1,0:T(8,128)(2,1)} %bitcast.19, bf16[8000,3584]{1,0:T(8,128)(2,1)} %param.10), kind=kOutput, calls=%fused_computation.3 | convolution fusion | flops 14682112000 | bytes 67372032 | tf_op jit(solution)/shard_map/dot_general | solution.py:49
  93.6 9.0 %gather_fusion.2 = f32[256]{0:T(256)S(1)} fusion(f32[256,8000]{0,1:T(8,128)} %get-tuple-element.15, s32[256]{0:T(256)S(1)} %bitcast.11), kind=kCustom, calls=%fused_computation.2 | custom fusion | bytes 4096 | tf_op jit(solution)/shard_map/jit(take_along_axis)/gather | solution.py:15
  102.6 0.1 gather.14
  102.7 0.1 select_select_fusion
  102.7 0.1 squeeze_stack_reshape.4
  102.8 38.9 %all-reduce.3 = (f32[4,64]{1,0:T(4,128)S(1)}, f32[4,64]{1,0:T(4,128)S(1)}, f32[4,64]{1,0:T(4,128)S(1)}) all-reduce(f32[4,64]{1,0:T(4,128)S(1)} %select_select_fusion, f32[4,64]{1,0:T(4,128)S(1)} %squeeze_stack_reshape.4, f32[4,64]{1,0:T(4,128)S(1)} %dynamic_update_slice.3), channel_id=1, replica_groups=mesh['dp'=4,'vocab'=8] {'dp','vocab'}, use_global_device_ids=true, to_apply=%region_0.1 | all-reduce | flops 768 | bytes 6144 | tf_op jit(solution)/shard_map/psum | solution.py:68
  141.8 0.1 fusion
  141.8 0.6 dynamic_slice.6
  142.4 0.7 slice_reduce_fusion
  143.7 0.6 fusion.4
  144.4 0.6 dynamic_slice.7
  (9 shorter events, 0.0 us)
Async XLA Ops:
  7.2 60.6 %all-gather.4.cloned.1.call-start = ((), (), s32[]{:S(2)}) async-start(), calls=%async_computation | async-start | bytes 2293760 | tf_op jit(solution)/shard_map/all_gather | solution.py:47
Sparse Core Ops, SparseCore 0:
  35.1 32.6 all-gather.3
where the time goes:
time: 154 us
  blocking collectives  85.1 us (55%)
  matrix products  25.9 us (17%)
  local copies, waits for them, and re-layouts  18.3 us (12%)
  between operations  17.8 us (12%)
  waiting for transfers between devices  4.07 us (3%)
  other arithmetic  2.34 us (2%)
    psum x1, blocking collectives, on_device(): lax.psum((partition, picked, ref_full), ('dp', 'vocab'))  38.9 us
    dot_general x1, matrix products, on_device(): lax.dot_general(portion.reshape(number * columns, model_width), head_weig...  25.9 us
    all_gather x1, blocking collectives, on_device(): whole_rows = lax.all_gather(combined, 'vocab', axis=2, tiled=True)  23.7 us
    gather x2, local copies, waits for them, and re-layouts, label_terms(): picked = jnp.take_along_axis(logits, clipped[:, None], axis=1)[:, 0]  9.07 us
    all_gather x1, blocking collectives, on_device(): lax.all_gather(token_mask, 'dp', axis=0, tiled=True)  7.92 us
    unnamed x1, blocking collectives  7.39 us
    all_gather x1, blocking collectives, on_device(): lax.all_gather(labels, 'dp', axis=0, tiled=True)  7.23 us
    all_gather x1, waiting for transfers between devices, on_device(): portion = lax.all_gather(whole_rows, 'dp', axis=0, tiled=True)  4.05 us
  transfers between devices with their start and end apart: 1, of which 1 were waited for; matrix products, arithmetic and copies ran while one was open for 3% of the time, Pallas kernels for 0%

commit v1 on v0

--- a/solution.py
+++ b/solution.py
@@ -6,6 +6,10 @@
 kto_beta = 0.1
 desirable_weight = 1.0
 undesirable_weight = 1.33
+
+
+def check_views(message, which_axis):
+    return jnp.concatenate(jax.lax.all_gather(message, which_axis), axis=2)
 
 
 def label_terms(logits, targets, first_row):
@@ -43,7 +47,7 @@
     seq_total = targets.shape[0]
     columns = targets.shape[1]
     combined = jnp.concatenate([hidden, kl_hidden], axis=1)
-    whole_rows = lax.all_gather(combined, "vocab", axis=2, tiled=True)
+    whole_rows = check_views(combined, "vocab")
     portion = lax.all_gather(whole_rows, "dp", axis=0, tiled=True)
     number = portion.shape[0]
     logits = lax.dot_general(

time: 154 us -> 147 us (0.955)
  blocking collectives: 85.1 us -> 78 us
  local copies, waits for them, and re-layouts: 18.3 us -> 16.7 us
    all_gather x1, blocking collectives: 23.7 us -> 16.5 us  [check_views(): return jnp.concatenate(jax.lax.all_gather(message, which_axis), axis=2)]
    all_gather x1 -> x0, local copies, waits for them, and re-layouts: 3.09 us -> none  [on_device(): whole_rows = lax.all_gather(combined, 'vocab', axis=2, tiled=True)]
    reshape x0 -> x2, local copies, waits for them, and re-layouts: none -> 1.62 us  [check_views(): return jnp.concatenate(jax.lax.all_gather(message, which_axis), axis=2)]
where the time goes in v1:
time: 147 us; the launch traced here: 146 us
  blocking collectives  78 us (53%)
  matrix products  25.8 us (18%)
  between operations  17.8 us (12%)
  local copies, waits for them, and re-layouts  16.7 us (11%)
  waiting for transfers between devices  5.58 us (4%)
  other arithmetic  2.34 us (2%)
    psum x1, blocking collectives, on_device(): lax.psum((partition, picked, ref_full), ('dp', 'vocab'))  39 us
    dot_general x1, matrix products, on_device(): lax.dot_general(portion.reshape(number * columns, model_width), head_weig...  25.8 us
    all_gather x1, blocking collectives, check_views(): return jnp.concatenate(jax.lax.all_gather(message, which_axis), axis=2)  16.5 us
    gather x2, local copies, waits for them, and re-layouts, label_terms(): picked = jnp.take_along_axis(logits, clipped[:, None], axis=1)[:, 0]  9.07 us
    all_gather x1, blocking collectives, on_device(): lax.all_gather(token_mask, 'dp', axis=0, tiled=True)  7.98 us
    unnamed x1, blocking collectives  7.37 us
    all_gather x1, blocking collectives, on_device(): lax.all_gather(labels, 'dp', axis=0, tiled=True)  7.17 us
    all_gather x1, waiting for transfers between devices, on_device(): portion = lax.all_gather(whole_rows, 'dp', axis=0, tiled=True)  5.57 us
  transfers between devices with their start and end apart: 1, of which 1 were waited for; matrix products, arithmetic and copies ran while one was open for 3% of the time, Pallas kernels for 0%

profile of v1, /device:TPU:0, one launch (start us, length us, event | category | flops | bytes accessed | tf_op | source)
XLA Modules:
  0.0 146.3 jit_solution(12750053764799776210)
XLA Ops:
  7.2 0.0 all-gather.5.cloned.1.call-start
  7.2 0.8 pad_maximum_fusion
  8.0 16.5 %all-gather = bf16[8,64,448]{2,1,0:T(8,128)(2,1)S(1)} all-gather(bf16[1,64,448]{2,1,0:T(8,128)(2,1)S(1)} %pad_maximum_fusion), channel_id=2, replica_groups=mesh['dp'=4,'vocab'=8] {'vocab'}, dimensions={0}, use_global_device_ids=true | all-gather | bytes 516096 | tf_op jit(solution)/shard_map/all_gather | solution.py:12
  24.5 0.3 copy.12
  24.8 1.3 reshape.71
  26.1 0.0 all-gather.5.cloned.1.call-update
  27.4 1.2 dynamic-slice
  28.7 0.8 dynamic-update-slice
  29.4 0.8 dynamic-update-slice.1
  30.2 7.4 %all-reduce.2 = (s32[4]{0:T(128)S(1)}, s32[4]{0:T(128)S(1)}) all-reduce(s32[4]{0:T(128)S(1)} %dynamic-update-slice, s32[4]{0:T(128)S(1)} %dynamic-update-slice.1), channel_id=1, replica_groups=mesh['dp'=4,'vocab'=8] {'dp'}, use_global_device_ids=true, to_apply=%add | all-reduce | flops 8 | bytes 64
  37.6 8.0 %all-gather.2 = s32[4,1,32]{2,1,0:T(1,128)S(1)} all-gather(s32[1,1,32]{2,1,0:T(1,128)} %bitcast.23), channel_id=1, replica_groups=mesh['dp'=4,'vocab'=8] {'dp'}, dimensions={0}, use_global_device_ids=true | all-gather | bytes 640 | tf_op jit(solution)/shard_map/all_gather | solution.py:41
  45.6 0.6 gather_fusion.1
  46.1 7.2 %all-gather.1 = s32[4,1,32]{2,1,0:T(1,128)S(1)} all-gather(s32[1,1,32]{2,1,0:T(1,128)} %bitcast.24), channel_id=1, replica_groups=mesh['dp'=4,'vocab'=8] {'dp'}, dimensions={0}, use_global_device_ids=true | all-gather | bytes 640 | tf_op jit(solution)/shard_map/all_gather | solution.py:40
  53.3 0.6 gather_fusion
  53.9 0.1 broadcast_clamp_fusion
  53.9 0.1 min.12
  54.0 0.8 dynamic_update_slice.3
  54.8 5.6 %all-gather.5.cloned.1.call-done = bf16[4,64,3584]{2,1,0:T(8,128)(2,1)} async-done(((bf16[1,64,3584]{2,1,0:T(8,128)(2,1)}), bf16[4,64,3584]{2,1,0:T(8,128)(2,1)}) %all-gather.5.cloned.1.call-update) | async-done | bytes 1835024 | tf_op jit(solution)/shard_map/all_gather | solution.py:51
  60.4 25.8 %exponential_reduce_fusion = (f32[256]{0:T(256)S(1)}, f32[256,8000]{0,1:T(8,128)}) fusion(bf16[256,3584]{1,0:T(8,128)(2,1)} %bitcast.25, bf16[8000,3584]{1,0:T(8,128)(2,1)} %param.10), kind=kOutput, calls=%fused_computation.3 | convolution fusion | flops 14682112000 | bytes 67372032 | tf_op jit(solution)/shard_map/dot_general | solution.py:53
  86.3 9.0 %gather_fusion.2 = f32[256]{0:T(256)S(1)} fusion(f32[256,8000]{0,1:T(8,128)} %get-tuple-element.15, s32[256]{0:T(256)S(1)} %bitcast.16), kind=kCustom, calls=%fused_computation.2 | custom fusion | bytes 4096 | tf_op jit(solution)/shard_map/jit(take_along_axis)/gather | solution.py:19
  95.3 0.1 gather.14
  95.3 0.1 select_select_fusion
  95.4 0.1 squeeze_stack_reshape.4
  95.5 39.0 %all-reduce.3 = (f32[4,64]{1,0:T(4,128)S(1)}, f32[4,64]{1,0:T(4,128)S(1)}, f32[4,64]{1,0:T(4,128)S(1)}) all-reduce(f32[4,64]{1,0:T(4,128)S(1)} %select_select_fusion, f32[4,64]{1,0:T(4,128)S(1)} %squeeze_stack_reshape.4, f32[4,64]{1,0:T(4,128)S(1)} %dynamic_update_slice.3), channel_id=1, replica_groups=mesh['dp'=4,'vocab'=8] {'dp','vocab'}, use_global_device_ids=true, to_apply=%region_0.1 | all-reduce | flops 768 | bytes 6144 | tf_op jit(solution)/shard_map/psum | solution.py:72
  134.5 0.1 fusion
  134.6 0.6 dynamic_slice.6
  135.1 0.7 slice_reduce_fusion
  136.5 0.6 fusion.4
  137.1 0.6 dynamic_slice.7
  (9 shorter events, 0.0 us)
Async XLA Ops:
  7.2 53.2 %all-gather.5.cloned.1.call-start = ((), (), s32[]{:S(2)}) async-start(), calls=%async_computation | async-start | bytes 2293760 | tf_op jit(solution)/shard_map/all_gather | solution.py:51
Sparse Core Ops, SparseCore 0:
  26.3 34.0 all-gather.4
